TPU v7x, 32 devices: a whole 2x2x4 slice. The times are simulated.
32 devices in a mesh: blk: 8 (over z, x), dp: 4 (over y, core).
Axes of the slice: x: 2, y: 2, z: 4, core: 2. Of those that a mesh axis runs over, the one named last changes fastest.
Arguments:
- embeddings: bfloat16 [8192, 512], P(('dp', 'blk')), may hold values from -16 to 16
- centers: bfloat16 [16384, 512], P(('blk', 'dp')), may hold values from -10 to 10
- labels: int32 [8192], P(('dp', 'blk')), may hold values from 0 to 16383
Outputs:
- loss: float32 [8192], P(('dp', 'blk'))
All inputs are finite; a program needn't handle non-finite values.
Results may differ from a plain program's by a relative error of at most 0.0017.
Values may be sent and summed in bfloat16 or wider, within the bound.
A program may use at most 128 MiB of HBM per device.

v0:
```python
import math
import jax
import jax.numpy as jnp
from jax import lax
from jax.sharding import PartitionSpec as P

EPSILON = 1e-06
LOGIT_SCALE = 30.0
MARGIN = 0.5


def unit_rows(matrix):
    values = matrix.astype(jnp.float32)
    return (values * lax.rsqrt(jnp.sum(values * values, axis=1, keepdims=True) + EPSILON)).astype(
        jnp.bfloat16
    )


def margin_loss(other_sum, target_cos):
    sine = jnp.sqrt(jnp.maximum(1.0 - target_cos * target_cos, 0.0))
    shifted = target_cos * math.cos(MARGIN) - sine * math.sin(MARGIN)
    return (
        LOGIT_SCALE
        + jnp.log(other_sum + jnp.exp(LOGIT_SCALE * shifted - LOGIT_SCALE))
        - LOGIT_SCALE * shifted
    )


def block_terms(rows, row_labels, centers_block, class_start):
    cosine = jnp.einsum("nd,cd->nc", rows, centers_block, preferred_element_type=jnp.float32)
    columns = class_start + jnp.arange(centers_block.shape[0], dtype=jnp.int32)
    is_target = row_labels[:, None] == columns[None, :]
    other_sum = jnp.sum(
        jnp.where(is_target, 0.0, jnp.exp(LOGIT_SCALE * cosine - LOGIT_SCALE)), axis=1
    )
    target_cos = jnp.sum(jnp.where(is_target, cosine, 0.0), axis=1)
    return (other_sum, target_cos)


def body(embeddings, centers, labels):
    emb_unit = unit_rows(embeddings)
    center_unit = unit_rows(centers)
    shard_classes = center_unit.shape[0]
    group_count = lax.axis_size("dp")
    group_index = lax.axis_index("dp")
    group_rows, group_labels = (
        lax.all_gather(emb_unit, "dp", axis=0, tiled=True),
        lax.all_gather(labels, "dp", axis=0, tiled=True),
    )
    group_total = group_rows.shape[0]
    zeros_sum = jnp.zeros((group_total,), jnp.float32)
    pieces = lax.all_gather(center_unit, "blk", axis=0, tiled=True)
    span_rows = math.gcd(math.gcd(pieces.shape[0], shard_classes), 512)

    def one_span(accum, step_index):
        first = step_index * span_rows
        block_rows = lax.dynamic_slice_in_dim(pieces, step_index * span_rows, span_rows, 0)
        class_start = (
            first // shard_classes * group_count + group_index
        ) * shard_classes + first % shard_classes
        other_part, target_part = block_terms(group_rows, group_labels, block_rows, class_start)
        return ((accum[0] + other_part, accum[1] + target_part), None)

    result, ignored = lax.scan(
        one_span, (zeros_sum, zeros_sum), jnp.arange(pieces.shape[0] // span_rows, dtype=jnp.int32)
    )
    other_group, target_group = result
    other_sum, target_cos = (
        lax.psum_scatter(other_group, "dp", scatter_dimension=0, tiled=True),
        lax.psum_scatter(target_group, "dp", scatter_dimension=0, tiled=True),
    )
    return margin_loss(other_sum, target_cos)


def solution(mesh):
    return jax.shard_map(
        body,
        mesh=mesh,
        in_specs=(P(("dp", "blk"), None), P(("blk", "dp"), None), P(("dp", "blk"))),
        out_specs=P(("dp", "blk")),
        check_vma=False,
    )
```

profile of v0, /device:TPU:0, one launch (start us, length us, event | category | flops | bytes accessed | tf_op | source)
XLA Modules:
  0.0 147.6 jit_solution(2375820200223989825)
XLA Ops:
  6.5 0.0 copy-start.1
  6.5 0.0 copy-start
  6.5 0.0 all-gather.6.cloned.1.call-start
  6.5 1.1 fusion.9
  7.7 1.8 %fusion.10 = bf16[256,512]{1,0:T(8,128)(2,1)} fusion(bf16[256,512]{1,0:T(8,128)(2,1)} %param.5, f32[256]{0:T(256)S(1)} %add_rsqrt_fusion.1), kind=kLoop, calls=%fused_computation.20 | loop fusion | flops 393216 | bytes 525312 | tf_op jit(solution)/shard_map/convert_element_type | solution.py:14
  9.4 0.0 all-gather.6.cloned.1.call-update
  9.5 0.0 all-gather.4.cloned.1.call-start
  9.5 1.2 fusion.7
  10.7 2.0 %fusion.8 = bf16[512,512]{1,0:T(8,128)(2,1)} fusion(bf16[512,512]{1,0:T(8,128)(2,1)} %param.6, f32[512]{0:T(512)S(1)} %add_rsqrt_fusion), kind=kLoop, calls=%fused_computation.16 | loop fusion | flops 786432 | bytes 1050624 | tf_op jit(solution)/shard_map/convert_element_type | solution.py:14
  12.7 0.0 all-gather.4.cloned.1.call-update
  12.8 0.0 copy-done.1
  12.8 0.6 dynamic-slice
  14.1 0.0 copy-done
  14.1 6.0 %all-gather = s32[4,1,256]{2,1,0:T(1,128)S(1)} all-gather(s32[1,1,256]{2,1,0:T(1,128)S(1)} %bitcast.21), channel_id=1, replica_groups=mesh['blk'=8,'dp'=4] {'dp'}, dimensions={0}, use_global_device_ids=true | all-gather | bytes 5120 | tf_op jit(solution)/shard_map/all_gather | solution.py:48
  20.1 8.9 %all-gather.6.cloned.1.call-done = bf16[1024,512]{1,0:T(8,128)(2,1)} async-done(((bf16[256,512]{1,0:T(8,128)(2,1)}), bf16[1024,512]{1,0:T(8,128)(2,1)}) %all-gather.6.cloned.1.call-update) | async-done | bytes 1048592 | tf_op jit(solution)/shard_map/all_gather | solution.py:47
  29.0 75.0 %all-gather.4.cloned.1.call-done = bf16[4096,512]{1,0:T(8,128)(2,1)} async-done(((bf16[512,512]{1,0:T(8,128)(2,1)}), bf16[4096,512]{1,0:T(8,128)(2,1)}) %all-gather.4.cloned.1.call-update) | async-done | bytes 4194320 | tf_op jit(solution)/shard_map/all_gather | solution.py:52
  104.0 30.3 %while.15 = (s32[]{:T(128)}, f32[1024]{0:T(1024)S(1)}, f32[1024]{0:T(1024)S(1)}, s32[1024]{0:T(1024)S(1)}, s32[8]{0:T(128)S(1)}, /*index=5*/s32[]{:T(128)}, bf16...) while((s32[]{:T(128)}, f32[1024]{0:T(1024)S(1)}, ...), condition=%wide.region_5.6_spmd.clone, body=%wide.region_2.5_spmd.clone.sunk | while | flops 540543488 | bytes 1614283 | solution.py:64
  104.0 0.6 dynamic_slice.22
  105.3 2.4 %fusion.18 = (f32[1024]{0:T(1024)S(1)}, f32[1024]{0:T(1024)S(1)}) fusion(s32[1024]{0:T(1024)S(1)} %get-tuple-element.256, s32[512]{0:T(512)S(1)} %iota_add_fusion.2, bf16[1024,512]{1,0:T(8,128)(2,1)} %get-tuple-element.260, bf16[4096,512]{1,0:T(8,128)(2,1)} %get-tuple-element.259, s32[]{:T(128)S(6)} %select_n.57), kind=kOutput, calls=%fused_computation.3.clone.1 | convolution fusion | flops 540538880 | bytes 1587204 | tf_op jit(solution)/shard_map/while/body/eval_jaxpr/nd,cd->nc/dot_general | solution.py:30
  107.8 0.6 dynamic_slice.22
  109.1 2.4 %fusion.18 = (f32[1024]{0:T(1024)S(1)}, f32[1024]{0:T(1024)S(1)}) fusion(s32[1024]{0:T(1024)S(1)} %get-tuple-element.256, s32[512]{0:T(512)S(1)} %iota_add_fusion.2, bf16[1024,512]{1,0:T(8,128)(2,1)} %get-tuple-element.260, bf16[4096,512]{1,0:T(8,128)(2,1)} %get-tuple-element.259, s32[]{:T(128)S(6)} %select_n.57), kind=kOutput, calls=%fused_computation.3.clone.1 | convolution fusion | flops 540538880 | bytes 1587204 | tf_op jit(solution)/shard_map/while/body/eval_jaxpr/nd,cd->nc/dot_general | solution.py:30
  111.6 0.6 dynamic_slice.22
  112.9 2.4 %fusion.18 = (f32[1024]{0:T(1024)S(1)}, f32[1024]{0:T(1024)S(1)}) fusion(s32[1024]{0:T(1024)S(1)} %get-tuple-element.256, s32[512]{0:T(512)S(1)} %iota_add_fusion.2, bf16[1024,512]{1,0:T(8,128)(2,1)} %get-tuple-element.260, bf16[4096,512]{1,0:T(8,128)(2,1)} %get-tuple-element.259, s32[]{:T(128)S(6)} %select_n.57), kind=kOutput, calls=%fused_computation.3.clone.1 | convolution fusion | flops 540538880 | bytes 1587204 | tf_op jit(solution)/shard_map/while/body/eval_jaxpr/nd,cd->nc/dot_general | solution.py:30
  115.4 0.6 dynamic_slice.22
  116.7 2.4 %fusion.18 = (f32[1024]{0:T(1024)S(1)}, f32[1024]{0:T(1024)S(1)}) fusion(s32[1024]{0:T(1024)S(1)} %get-tuple-element.256, s32[512]{0:T(512)S(1)} %iota_add_fusion.2, bf16[1024,512]{1,0:T(8,128)(2,1)} %get-tuple-element.260, bf16[4096,512]{1,0:T(8,128)(2,1)} %get-tuple-element.259, s32[]{:T(128)S(6)} %select_n.57), kind=kOutput, calls=%fused_computation.3.clone.1 | convolution fusion | flops 540538880 | bytes 1587204 | tf_op jit(solution)/shard_map/while/body/eval_jaxpr/nd,cd->nc/dot_general | solution.py:30
  119.2 0.6 dynamic_slice.22
  120.5 2.4 %fusion.18 = (f32[1024]{0:T(1024)S(1)}, f32[1024]{0:T(1024)S(1)}) fusion(s32[1024]{0:T(1024)S(1)} %get-tuple-element.256, s32[512]{0:T(512)S(1)} %iota_add_fusion.2, bf16[1024,512]{1,0:T(8,128)(2,1)} %get-tuple-element.260, bf16[4096,512]{1,0:T(8,128)(2,1)} %get-tuple-element.259, s32[]{:T(128)S(6)} %select_n.57), kind=kOutput, calls=%fused_computation.3.clone.1 | convolution fusion | flops 540538880 | bytes 1587204 | tf_op jit(solution)/shard_map/while/body/eval_jaxpr/nd,cd->nc/dot_general | solution.py:30
  123.0 0.6 dynamic_slice.22
  124.3 2.4 %fusion.18 = (f32[1024]{0:T(1024)S(1)}, f32[1024]{0:T(1024)S(1)}) fusion(s32[1024]{0:T(1024)S(1)} %get-tuple-element.256, s32[512]{0:T(512)S(1)} %iota_add_fusion.2, bf16[1024,512]{1,0:T(8,128)(2,1)} %get-tuple-element.260, bf16[4096,512]{1,0:T(8,128)(2,1)} %get-tuple-element.259, s32[]{:T(128)S(6)} %select_n.57), kind=kOutput, calls=%fused_computation.3.clone.1 | convolution fusion | flops 540538880 | bytes 1587204 | tf_op jit(solution)/shard_map/while/body/eval_jaxpr/nd,cd->nc/dot_general | solution.py:30
  126.8 0.6 dynamic_slice.22
  128.1 2.4 %fusion.18 = (f32[1024]{0:T(1024)S(1)}, f32[1024]{0:T(1024)S(1)}) fusion(s32[1024]{0:T(1024)S(1)} %get-tuple-element.256, s32[512]{0:T(512)S(1)} %iota_add_fusion.2, bf16[1024,512]{1,0:T(8,128)(2,1)} %get-tuple-element.260, bf16[4096,512]{1,0:T(8,128)(2,1)} %get-tuple-element.259, s32[]{:T(128)S(6)} %select_n.57), kind=kOutput, calls=%fused_computation.3.clone.1 | convolution fusion | flops 540538880 | bytes 1587204 | tf_op jit(solution)/shard_map/while/body/eval_jaxpr/nd,cd->nc/dot_general | solution.py:30
  130.5 0.6 dynamic_slice.22
  131.9 2.4 %fusion.18 = (f32[1024]{0:T(1024)S(1)}, f32[1024]{0:T(1024)S(1)}) fusion(s32[1024]{0:T(1024)S(1)} %get-tuple-element.256, s32[512]{0:T(512)S(1)} %iota_add_fusion.2, bf16[1024,512]{1,0:T(8,128)(2,1)} %get-tuple-element.260, bf16[4096,512]{1,0:T(8,128)(2,1)} %get-tuple-element.259, s32[]{:T(128)S(6)} %select_n.57), kind=kOutput, calls=%fused_computation.3.clone.1 | convolution fusion | flops 540538880 | bytes 1587204 | tf_op jit(solution)/shard_map/while/body/eval_jaxpr/nd,cd->nc/dot_general | solution.py:30
  134.3 5.8 %all-reduce.2 = (f32[1024]{0:T(1024)S(1)}, f32[1024]{0:T(1024)S(1)}) all-reduce(f32[1024]{0:T(1024)S(1)} %get-tuple-element.111, f32[1024]{0:T(1024)S(1)} %get-tuple-element.112), channel_id=2, replica_groups=mesh['blk'=8,'dp'=4] {'dp'}, use_global_device_ids=true, to_apply=%region_6.7.clone | all-reduce | flops 2048 | bytes 16384
  140.1 0.7 fusion.13
  (21 shorter events, 0.1 us)
Async XLA Ops:
  6.5 6.3 %copy-start.1 = (u32[32]{0:T(128)S(1)}, u32[32]{0:T(128)}, u32[]{:S(2)}) copy-start(u32[32]{0:T(128)} %constant.103) | copy-start | bytes 388
  6.5 7.5 %copy-start = (s32[256]{0:T(256)S(1)}, s32[256]{0:T(256)}, u32[]{:S(2)}) copy-start(s32[256]{0:T(256)} %param.7) | copy-start | bytes 3076
  6.5 22.5 %all-gather.6.cloned.1.call-start = ((), (), s32[]{:S(2)}) async-start(), calls=%async_computation.1 | async-start | bytes 1310720 | tf_op jit(solution)/shard_map/all_gather | solution.py:47
  9.5 94.5 %all-gather.4.cloned.1.call-start = ((), (), s32[]{:S(2)}) async-start(), calls=%async_computation | async-start | bytes 4718592 | tf_op jit(solution)/shard_map/all_gather | solution.py:52
Sparse Core Ops, SparseCore 0:
  9.6 19.4 all-gather.5
  31.2 72.7 all-gather.3
where the time goes:
time: 148 us
  waiting for transfers between devices  83.9 us (57%)
  matrix products  19.6 us (13%)
  between operations  14.1 us (10%)
  blocking collectives  11.8 us (8%)
  other arithmetic  6.88 us (5%)
  loops' own time  5.78 us (4%)
  local copies, waits for them, and re-layouts  5.52 us (4%)
    all_gather x1, waiting for transfers between devices, body(): pieces = lax.all_gather(center_unit, 'blk', axis=0, tiled=True)  75 us
    dot_general x8, matrix products, block_terms(): jnp.einsum('nd,cd->nc', rows, centers_block, preferred_element_type=jnp.f...  19.6 us
    all_gather x1, waiting for transfers between devices, body(): lax.all_gather(emb_unit, 'dp', axis=0, tiled=True)  8.92 us
    all_gather x1, blocking collectives, body(): lax.all_gather(labels, 'dp', axis=0, tiled=True)  6.04 us
    another operation x1, loops' own time, body(): lax.scan(one_span, (zeros_sum, zeros_sum), jnp.arange(pieces.shape[0] //...  5.78 us
    unnamed x1, blocking collectives  5.77 us
    dynamic_slice x8, local copies, waits for them, and re-layouts, body(): lax.scan(one_span, (zeros_sum, zeros_sum), jnp.arange(pieces.shape[0] //...  4.9 us
    convert_element_type x2, other arithmetic, unit_rows(): (values * lax.rsqrt(jnp.sum(values * values, axis=1, keepdims=True) + EPS...  3.79 us
  transfers between devices with their start and end apart: 2, of which 2 were waited for; matrix products, arithmetic and copies ran while one was open for 3% of the time, Pallas kernels for 0%

commit v1 on v0

--- a/solution.py
+++ b/solution.py
@@ -49,7 +49,12 @@
     )
     group_total = group_rows.shape[0]
     zeros_sum = jnp.zeros((group_total,), jnp.float32)
-    pieces = lax.all_gather(center_unit, "blk", axis=0, tiled=True)
+    ring = [center_unit]
+    for hop in range(7):
+        ring.append(lax.ppermute(ring[-1], "blk", [(dev, (dev + 1) % 8) for dev in range(8)]))
+    pieces = jnp.roll(
+        jnp.concatenate(ring[::-1], axis=0), (lax.axis_index("blk") + 1) * ring[0].shape[0], axis=0
+    )
     span_rows = math.gcd(math.gcd(pieces.shape[0], shard_classes), 512)
 
     def one_span(accum, step_index):

time: 148 us -> 163 us (1.10)
  local copies, waits for them, and re-layouts: 5.52 us -> 13.4 us
  waiting for transfers between devices: 83.9 us -> 88.3 us
  starting transfers between devices: 0.04 us -> 3.04 us
    ppermute x0 -> x7, waiting for transfers between devices: none -> 87.6 us  [body(): lax.ppermute(ring[-1], 'blk', [(dev, (dev + 1) % 8) for dev in range(8)])]
    all_gather x1 -> x0, waiting for transfers between devices: 75 us -> none  [body(): pieces = lax.all_gather(center_unit, 'blk', axis=0, tiled=True)]
    all_gather x1, waiting for transfers between devices: 8.92 us -> 0.7 us  [body(): lax.all_gather(emb_unit, 'dp', axis=0, tiled=True)]
    unnamed x5 -> x17, local copies, waits for them, and re-layouts: 0.62 us -> 5.93 us
    ppermute x0 -> x7, starting transfers between devices: none -> 3.04 us  [body(): lax.ppermute(ring[-1], 'blk', [(dev, (dev + 1) % 8) for dev in range(8)])]
    dynamic_slice x0 -> x1, local copies, waits for them, and re-layouts: none -> 2.22 us  [body(): jnp.roll(jnp.concatenate(ring[::-1], axis=0), (lax.axis_index('blk') + 1)...]
  transfers between devices with their start and end apart: 2 -> 8, of which waited for: 2 -> 8; matrix products, arithmetic and copies ran while one was open for 3% -> 7% of each run, Pallas kernels for 0% -> 0%
where the time goes in v1:
time: 163 us; the launch traced here: 162 us
  waiting for transfers between devices  88.3 us (54%)
  matrix products  19.6 us (12%)
  between operations  14.2 us (9%)
  local copies, waits for them, and re-layouts  13.4 us (8%)
  blocking collectives  11.3 us (7%)
  other arithmetic  6.46 us (4%)
  loops' own time  5.79 us (4%)
  starting transfers between devices  3.04 us (2%)
    ppermute x7, waiting for transfers between devices, body(): lax.ppermute(ring[-1], 'blk', [(dev, (dev + 1) % 8) for dev in range(8)])  87.6 us
    dot_general x8, matrix products, block_terms(): jnp.einsum('nd,cd->nc', rows, centers_block, preferred_element_type=jnp.f...  19.6 us
    unnamed x1, blocking collectives  6 us
    unnamed x17, local copies, waits for them, and re-layouts  5.93 us
    another operation x1, loops' own time, body(): lax.scan(one_span, (zeros_sum, zeros_sum), jnp.arange(pieces.shape[0] //...  5.79 us
    all_gather x1, blocking collectives, body(): lax.all_gather(labels, 'dp', axis=0, tiled=True)  5.28 us
    dynamic_slice x8, local copies, waits for them, and re-layouts, body(): lax.scan(one_span, (zeros_sum, zeros_sum), jnp.arange(pieces.shape[0] //...  5.22 us
  transfers between devices with their start and end apart: 8, of which 8 were waited for; matrix products, arithmetic and copies ran while one was open for 7% of the time, Pallas kernels for 0%

profile of v1, /device:TPU:0, one launch (start us, length us, event | category | flops | bytes accessed | tf_op | source)
XLA Modules:
  0.0 162.0 jit_solution(17804812616271669002)
XLA Ops:
  6.5 1.3 fusion.7
  7.8 1.2 fusion.8
  9.1 3.0 %collective-permute-start = (bf16[512,512]{1,0:T(8,128)(2,1)S(1)}, bf16[512,512]{1,0:T(8,128)(2,1)S(1)}, u32[]{:S(2)}, u32[]{:S(2)}) collective-permute-start(bf16[512,512]{1,0:T(8,128)(2,1)S(1)} %fusion.8), channel_id=1, source_target_pairs={{0,4},{4,8},{8,12},{12,16},{16,20},{20,24},{24,28},{28,0},{1,5},{5... | collective-permute-start | bytes 1572872 | tf_op jit(solution)/shard_map/ppermute | solution.py:54
  12.1 15.0 %collective-permute-done = bf16[512,512]{1,0:T(8,128)(2,1)S(1)} collective-permute-done((bf16[512,512]{1,0:T(8,128)(2,1)S(1)}, bf16[512,512]{1,0:T(8,128)(2,1)S(1)}, u32[]{:S(2)}, u32[]{:S(2)}) %collective-permute-start) | collective-permute-done | bytes 524320 | tf_op jit(solution)/shard_map/ppermute | solution.py:54
  27.0 0.0 collective-permute-start.1
  27.0 15.8 %collective-permute-done.1 = bf16[512,512]{1,0:T(8,128)(2,1)S(1)} collective-permute-done((bf16[512,512]{1,0:T(8,128)(2,1)S(1)}, bf16[512,512]{1,0:T(8,128)(2,1)S(1)}, u32[]{:S(2)}, u32[]{:S(2)}) %collective-permute-start.1) | collective-permute-done | bytes 524320 | tf_op jit(solution)/shard_map/ppermute | solution.py:54
  42.8 0.0 collective-permute-start.2
  42.8 14.9 %collective-permute-done.2 = bf16[512,512]{1,0:T(8,128)(2,1)S(1)} collective-permute-done((bf16[512,512]{1,0:T(8,128)(2,1)S(1)}, bf16[512,512]{1,0:T(8,128)(2,1)S(1)}, u32[]{:S(2)}, u32[]{:S(2)}) %collective-permute-start.2) | collective-permute-done | bytes 524320 | tf_op jit(solution)/shard_map/ppermute | solution.py:54
  57.7 0.0 collective-permute-start.3
  57.8 14.1 %collective-permute-done.3 = bf16[512,512]{1,0:T(8,128)(2,1)S(1)} collective-permute-done((bf16[512,512]{1,0:T(8,128)(2,1)S(1)}, bf16[512,512]{1,0:T(8,128)(2,1)S(1)}, u32[]{:S(2)}, u32[]{:S(2)}) %collective-permute-start.3) | collective-permute-done | bytes 524320 | tf_op jit(solution)/shard_map/ppermute | solution.py:54
  71.8 0.0 collective-permute-start.4
  71.8 13.2 %collective-permute-done.4 = bf16[512,512]{1,0:T(8,128)(2,1)S(1)} collective-permute-done((bf16[512,512]{1,0:T(8,128)(2,1)S(1)}, bf16[512,512]{1,0:T(8,128)(2,1)S(1)}, u32[]{:S(2)}, u32[]{:S(2)}) %collective-permute-start.4) | collective-permute-done | bytes 524320 | tf_op jit(solution)/shard_map/ppermute | solution.py:54
  85.0 0.0 collective-permute-start.5
  85.0 12.5 %collective-permute-done.5 = bf16[512,512]{1,0:T(8,128)(2,1)} collective-permute-done((bf16[512,512]{1,0:T(8,128)(2,1)S(1)}, bf16[512,512]{1,0:T(8,128)(2,1)}, u32[]{:S(2)}, u32[]{:S(2)}) %collective-permute-start.5) | collective-permute-done | bytes 524320 | tf_op jit(solution)/shard_map/ppermute | solution.py:54
  97.5 0.0 collective-permute-start.6
  97.5 1.1 fusion.9
  98.6 1.8 %fusion.10 = bf16[256,512]{1,0:T(8,128)(2,1)} fusion(bf16[256,512]{1,0:T(8,128)(2,1)} %param.5, f32[256]{0:T(256)S(1)} %add_rsqrt_fusion.1), kind=kLoop, calls=%fused_computation.20 | loop fusion | flops 393216 | bytes 525312 | tf_op jit(solution)/shard_map/convert_element_type | solution.py:14
  100.4 0.0 all-gather.3.cloned.1.call-update
  100.5 1.2 dynamic-slice
  102.3 5.3 %all-gather = s32[4,1,256]{2,1,0:T(1,128)S(1)} all-gather(s32[1,1,256]{2,1,0:T(1,128)} %bitcast.21), channel_id=1, replica_groups=mesh['blk'=8,'dp'=4] {'dp'}, dimensions={0}, use_global_device_ids=true | all-gather | bytes 5120 | tf_op jit(solution)/shard_map/all_gather | solution.py:48
  107.5 2.2 %collective-permute-done.6 = bf16[512,512]{1,0:T(8,128)(2,1)} collective-permute-done((bf16[512,512]{1,0:T(8,128)(2,1)}, bf16[512,512]{1,0:T(8,128)(2,1)}, u32[]{:S(2)}, u32[]{:S(2)}) %collective-permute-start.6) | collective-permute-done | bytes 524320 | tf_op jit(solution)/shard_map/ppermute | solution.py:54
  109.7 1.1 constant_dynamic-update-slice_fusion.15
  110.8 1.1 constant_dynamic-update-slice_fusion.14
  112.1 0.2 constant_dynamic-update-slice_fusion.8
  112.3 1.1 constant_dynamic-update-slice_fusion.7
  113.3 1.1 constant_dynamic-update-slice_fusion.6
  114.7 0.2 constant_dynamic-update-slice_fusion
  114.8 2.2 %constant_dynamic-slice_fusion = bf16[4096,512]{1,0:T(8,128)(2,1)} fusion(bf16[8192,512]{1,0:T(8,128)(2,1)S(1)} %constant_dynamic-update-slice_fusion, s32[]{:T(128)S(6)} %select_n.52), kind=kLoop, calls=%fused_computation.43 | loop fusion | bytes 8388612 | tf_op jit(solution)/shard_map/jit(_roll_dynamic)/dynamic_slice | solution.py:55
  117.0 0.7 all-gather.3.cloned.1.call-done
  117.8 30.7 %while.15 = (s32[]{:T(128)}, f32[1024]{0:T(1024)S(1)}, f32[1024]{0:T(1024)S(1)}, s32[1024]{0:T(1024)S(1)}, s32[8]{0:T(128)S(1)}, /*index=5*/s32[]{:T(128)}, bf16...) while((s32[]{:T(128)}, f32[1024]{0:T(1024)S(1)}, ...), condition=%wide.region_5.6_spmd.clone, body=%wide.region_2.5_spmd.clone.sunk | while | flops 540543488 | bytes 1614283 | solution.py:69
  117.8 0.7 dynamic_slice.28
  119.1 2.5 %fusion.18 = (f32[1024]{0:T(1024)S(1)}, f32[1024]{0:T(1024)S(1)}) fusion(s32[1024]{0:T(1024)S(1)} %get-tuple-element.256, s32[512]{0:T(512)S(1)} %iota_add_fusion.2, bf16[1024,512]{1,0:T(8,128)(2,1)} %get-tuple-element.260, bf16[4096,512]{1,0:T(8,128)(2,1)} %get-tuple-element.259, s32[]{:T(128)S(6)} %select_n.71), kind=kOutput, calls=%fused_computation.3.clone.1 | convolution fusion | flops 540538880 | bytes 1587204 | tf_op jit(solution)/shard_map/while/body/eval_jaxpr/nd,cd->nc/dot_general | solution.py:30
  121.6 0.7 dynamic_slice.28
  122.9 2.4 %fusion.18 = (f32[1024]{0:T(1024)S(1)}, f32[1024]{0:T(1024)S(1)}) fusion(s32[1024]{0:T(1024)S(1)} %get-tuple-element.256, s32[512]{0:T(512)S(1)} %iota_add_fusion.2, bf16[1024,512]{1,0:T(8,128)(2,1)} %get-tuple-element.260, bf16[4096,512]{1,0:T(8,128)(2,1)} %get-tuple-element.259, s32[]{:T(128)S(6)} %select_n.71), kind=kOutput, calls=%fused_computation.3.clone.1 | convolution fusion | flops 540538880 | bytes 1587204 | tf_op jit(solution)/shard_map/while/body/eval_jaxpr/nd,cd->nc/dot_general | solution.py:30
  125.4 0.7 dynamic_slice.28
  126.8 2.5 %fusion.18 = (f32[1024]{0:T(1024)S(1)}, f32[1024]{0:T(1024)S(1)}) fusion(s32[1024]{0:T(1024)S(1)} %get-tuple-element.256, s32[512]{0:T(512)S(1)} %iota_add_fusion.2, bf16[1024,512]{1,0:T(8,128)(2,1)} %get-tuple-element.260, bf16[4096,512]{1,0:T(8,128)(2,1)} %get-tuple-element.259, s32[]{:T(128)S(6)} %select_n.71), kind=kOutput, calls=%fused_computation.3.clone.1 | convolution fusion | flops 540538880 | bytes 1587204 | tf_op jit(solution)/shard_map/while/body/eval_jaxpr/nd,cd->nc/dot_general | solution.py:30
  129.3 0.7 dynamic_slice.28
  130.6 2.4 %fusion.18 = (f32[1024]{0:T(1024)S(1)}, f32[1024]{0:T(1024)S(1)}) fusion(s32[1024]{0:T(1024)S(1)} %get-tuple-element.256, s32[512]{0:T(512)S(1)} %iota_add_fusion.2, bf16[1024,512]{1,0:T(8,128)(2,1)} %get-tuple-element.260, bf16[4096,512]{1,0:T(8,128)(2,1)} %get-tuple-element.259, s32[]{:T(128)S(6)} %select_n.71), kind=kOutput, calls=%fused_computation.3.clone.1 | convolution fusion | flops 540538880 | bytes 1587204 | tf_op jit(solution)/shard_map/while/body/eval_jaxpr/nd,cd->nc/dot_general | solution.py:30
  133.1 0.7 dynamic_slice.28
  134.5 2.5 %fusion.18 = (f32[1024]{0:T(1024)S(1)}, f32[1024]{0:T(1024)S(1)}) fusion(s32[1024]{0:T(1024)S(1)} %get-tuple-element.256, s32[512]{0:T(512)S(1)} %iota_add_fusion.2, bf16[1024,512]{1,0:T(8,128)(2,1)} %get-tuple-element.260, bf16[4096,512]{1,0:T(8,128)(2,1)} %get-tuple-element.259, s32[]{:T(128)S(6)} %select_n.71), kind=kOutput, calls=%fused_computation.3.clone.1 | convolution fusion | flops 540538880 | bytes 1587204 | tf_op jit(solution)/shard_map/while/body/eval_jaxpr/nd,cd->nc/dot_general | solution.py:30
  137.0 0.7 dynamic_slice.28
  138.3 2.4 %fusion.18 = (f32[1024]{0:T(1024)S(1)}, f32[1024]{0:T(1024)S(1)}) fusion(s32[1024]{0:T(1024)S(1)} %get-tuple-element.256, s32[512]{0:T(512)S(1)} %iota_add_fusion.2, bf16[1024,512]{1,0:T(8,128)(2,1)} %get-tuple-element.260, bf16[4096,512]{1,0:T(8,128)(2,1)} %get-tuple-element.259, s32[]{:T(128)S(6)} %select_n.71), kind=kOutput, calls=%fused_computation.3.clone.1 | convolution fusion | flops 540538880 | bytes 1587204 | tf_op jit(solution)/shard_map/while/body/eval_jaxpr/nd,cd->nc/dot_general | solution.py:30
  140.8 0.7 dynamic_slice.28
  142.1 2.5 %fusion.18 = (f32[1024]{0:T(1024)S(1)}, f32[1024]{0:T(1024)S(1)}) fusion(s32[1024]{0:T(1024)S(1)} %get-tuple-element.256, s32[512]{0:T(512)S(1)} %iota_add_fusion.2, bf16[1024,512]{1,0:T(8,128)(2,1)} %get-tuple-element.260, bf16[4096,512]{1,0:T(8,128)(2,1)} %get-tuple-element.259, s32[]{:T(128)S(6)} %select_n.71), kind=kOutput, calls=%fused_computation.3.clone.1 | convolution fusion | flops 540538880 | bytes 1587204 | tf_op jit(solution)/shard_map/while/body/eval_jaxpr/nd,cd->nc/dot_general | solution.py:30
  144.6 0.7 dynamic_slice.28
  146.0 2.4 %fusion.18 = (f32[1024]{0:T(1024)S(1)}, f32[1024]{0:T(1024)S(1)}) fusion(s32[1024]{0:T(1024)S(1)} %get-tuple-element.256, s32[512]{0:T(512)S(1)} %iota_add_fusion.2, bf16[1024,512]{1,0:T(8,128)(2,1)} %get-tuple-element.260, bf16[4096,512]{1,0:T(8,128)(2,1)} %get-tuple-element.259, s32[]{:T(128)S(6)} %select_n.71), kind=kOutput, calls=%fused_computation.3.clone.1 | convolution fusion | flops 540538880 | bytes 1587204 | tf_op jit(solution)/shard_map/while/body/eval_jaxpr/nd,cd->nc/dot_general | solution.py:30
  148.5 6.0 %all-reduce.2 = (f32[1024]{0:T(1024)S(1)}, f32[1024]{0:T(1024)S(1)}) all-reduce(f32[1024]{0:T(1024)S(1)} %get-tuple-element.111, f32[1024]{0:T(1024)S(1)} %get-tuple-element.112), channel_id=2, replica_groups=mesh['blk'=8,'dp'=4] {'dp'}, use_global_device_ids=true, to_apply=%region_6.7.clone | all-reduce | flops 2048 | bytes 16384
  154.5 0.7 fusion.13
  (34 shorter events, 0.5 us)
Async XLA Ops:
  6.5 105.6 %copy-start = (bf16[512,512]{1,0:T(8,128)(2,1)S(1)}, bf16[512,512]{1,0:T(8,128)(2,1)}, u32[]{:S(2)}) copy-start(bf16[512,512]{1,0:T(8,128)(2,1)} %param.6) | copy-start | bytes 1572868
  6.5 111.2 %all-gather.3.cloned.1.call-start = ((), (), s32[]{:S(2)}) async-start(), calls=%async_computation | async-start | bytes 1310720 | tf_op jit(solution)/shard_map/all_gather | solution.py:47
  9.1 18.0 %collective-permute-start = (bf16[512,512]{1,0:T(8,128)(2,1)S(1)}, bf16[512,512]{1,0:T(8,128)(2,1)S(1)}, u32[]{:S(2)}, u32[]{:S(2)}) collective-permute-start(bf16[512,512]{1,0:T(8,128)(2,1)S(1)} %fusion.8), channel_id=1, source_target_pairs={{0,4},{4,8},{8,12},{12,16},{16,20},{20,24},{24,28},{28,0},{1,5},{5... | collective-permute-start | bytes 1572872 | tf_op jit(solution)/shard_map/ppermute | solution.py:54
  27.0 15.8 %collective-permute-start.1 = (bf16[512,512]{1,0:T(8,128)(2,1)S(1)}, bf16[512,512]{1,0:T(8,128)(2,1)S(1)}, u32[]{:S(2)}, u32[]{:S(2)}) collective-permute-start(bf16[512,512]{1,0:T(8,128)(2,1)S(1)} %collective-permute-done), channel_id=1, source_target_pairs={{0,4},{4,8},{8,12},{12,16},{16,20},{20,24},{24,28},{28,0},{1,5},{5... | collective-permute-start | bytes 1572872 | tf_op jit(solution)/shard_map/ppermute | solution.py:54
  42.8 14.9 %collective-permute-start.2 = (bf16[512,512]{1,0:T(8,128)(2,1)S(1)}, bf16[512,512]{1,0:T(8,128)(2,1)S(1)}, u32[]{:S(2)}, u32[]{:S(2)}) collective-permute-start(bf16[512,512]{1,0:T(8,128)(2,1)S(1)} %collective-permute-done.1), channel_id=1, source_target_pairs={{0,4},{4,8},{8,12},{12,16},{16,20},{20,24},{24,28},{28,0},{1,5},{5... | collective-permute-start | bytes 1572872 | tf_op jit(solution)/shard_map/ppermute | solution.py:54
  57.7 14.1 %collective-permute-start.3 = (bf16[512,512]{1,0:T(8,128)(2,1)S(1)}, bf16[512,512]{1,0:T(8,128)(2,1)S(1)}, u32[]{:S(2)}, u32[]{:S(2)}) collective-permute-start(bf16[512,512]{1,0:T(8,128)(2,1)S(1)} %collective-permute-done.2), channel_id=1, source_target_pairs={{0,4},{4,8},{8,12},{12,16},{16,20},{20,24},{24,28},{28,0},{1,5},{5... | collective-permute-start | bytes 1572872 | tf_op jit(solution)/shard_map/ppermute | solution.py:54
  71.8 13.2 %collective-permute-start.4 = (bf16[512,512]{1,0:T(8,128)(2,1)S(1)}, bf16[512,512]{1,0:T(8,128)(2,1)S(1)}, u32[]{:S(2)}, u32[]{:S(2)}) collective-permute-start(bf16[512,512]{1,0:T(8,128)(2,1)S(1)} %collective-permute-done.3), channel_id=1, source_target_pairs={{0,4},{4,8},{8,12},{12,16},{16,20},{20,24},{24,28},{28,0},{1,5},{5... | collective-permute-start | bytes 1572872 | tf_op jit(solution)/shard_map/ppermute | solution.py:54
  85.0 12.5 %collective-permute-start.5 = (bf16[512,512]{1,0:T(8,128)(2,1)S(1)}, bf16[512,512]{1,0:T(8,128)(2,1)}, u32[]{:S(2)}, u32[]{:S(2)}) collective-permute-start(bf16[512,512]{1,0:T(8,128)(2,1)S(1)} %collective-permute-done.4), channel_id=1, source_target_pairs={{0,4},{4,8},{8,12},{12,16},{16,20},{20,24},{24,28},{28,0},{1,5},{5... | collective-permute-start | bytes 1572872 | tf_op jit(solution)/shard_map/ppermute | solution.py:54
  97.5 12.2 %collective-permute-start.6 = (bf16[512,512]{1,0:T(8,128)(2,1)}, bf16[512,512]{1,0:T(8,128)(2,1)}, u32[]{:S(2)}, u32[]{:S(2)}) collective-permute-start(bf16[512,512]{1,0:T(8,128)(2,1)} %collective-permute-done.5), channel_id=1, source_target_pairs={{0,4},{4,8},{8,12},{12,16},{16,20},{20,24},{24,28},{28,0},{1,5},{5... | collective-permute-start | bytes 1572872 | tf_op jit(solution)/shard_map/ppermute | solution.py:54
Sparse Core Ops, SparseCore 0:
  100.5 17.1 all-gather.2
